TPU v7x, 32 devices: a whole 2x2x4 slice. The times are simulated.
32 devices in a mesh: dp: 4 (over y, x), expert: 8 (over z, core).
Axes of the slice: x: 2, y: 2, z: 4, core: 2. Of those that a mesh axis runs over, the one named last changes fastest.
Arguments:
- out_grad: bfloat16 [384, 3072], P(('dp', 'expert')), may hold values from -6 to 6
- layer_input: bfloat16 [384, 3072], P(('dp', 'expert')), may hold values from -6 to 6
- expert_ids: int32 [384, 2], P(('dp', 'expert')), may hold values from 0 to 7, as said below
- gate_prob: float32 [384, 2], P(('dp', 'expert')), may hold values from 0.05 to 1
- w_stack: bfloat16 [3, 3072, 8192], P(None, 'dp', 'expert'), may hold values from -0.109375 to 0.109375
- scale_exps: int32 [3, 24, 64], P(None, 'dp', 'expert'), may hold values from -1 to 1
Outputs:
- input_grad: bfloat16 [384, 3072], P(('dp', 'expert'))
- weight_grads: float32 [3, 3072, 8192], P(None, 'dp', 'expert')
Inputs may be any that keep to these rules, and one draw needn't show every extreme that they name: `expert_ids`: each row names two different experts. In each aligned block of 12 rows (the tokens of one device) between 1 and 3 rows name expert 0, and some blocks have exactly 3 in every draw.
All inputs are finite; a program needn't handle non-finite values.
Results may differ from a plain program's by a relative error of at most 0.015.
Values may be sent and summed in bfloat16 or wider, within the bound.
A program may use at most 128 MiB of HBM per device.

v0:
```python
import functools

import jax
import jax.numpy as jnp
from jax import lax
from jax.experimental import pallas as pl
from jax.experimental.pallas import tpu as pltpu
from jax.sharding import PartitionSpec as P

TILE = 128
CAP = 3
DIRECT = 64
TALL = 256
BF = jnp.bfloat16
F32 = jnp.float32
VMEM_LIMIT = 60 * 1024 * 1024


def iota(shape, dim):
    return lax.broadcasted_iota(jnp.int32, shape, dim)


def mm(a, b, ca=1, cb=0):
    return lax.dot_general(a, b, (((ca,), (cb,)), ((), ())), preferred_element_type=F32)


def exchange_kernel(
    n_dp, n_ex, chunk,
    og_ref, li_ref, ids_ref, prob_ref, exps_ref, w_hbm,
    xt_ref, act_ref, ig_ref,
    w, slab_out, slabs, x, part_out, part_in, acts, hids, acc, back_out, back_in, own_out, own_in,
    w_sem, s1_send, s1_recv, s2_send, s2_recv, s3_send, s3_recv, rs_send, rs_recv,
    ag_send, ag_recv, hg_send, hg_recv, b1_send, b1_recv, b2_send, b2_recv,
):
    p, e = lax.axis_index("dp"), lax.axis_index("expert")
    tok, width = og_ref.shape
    _, depth, hid = w.shape
    rows = n_ex * CAP
    n_chunk = hid // chunk
    pairs = n_ex // 2
    z, core = e // 2, e % 2
    partner = 2 * z + 1 - core

    def send(src, dst, ssem, rsem, q, f):
        copy = pltpu.make_async_remote_copy(
            src_ref=src, dst_ref=dst, send_sem=ssem, recv_sem=rsem,
            device_id=(q, f), device_id_type=pl.DeviceIdType.MESH,
        )
        copy.start()
        return copy

    w_copies = [
        pltpu.make_async_copy(w_hbm.at[m], w.at[m], w_sem.at[m]) for m in range(3)
    ]
    for copy in w_copies:
        copy.start()

    barrier = pltpu.get_barrier_semaphore()
    for k in range(1, n_dp):
        pl.semaphore_signal(
            barrier, inc=1, device_id=(lax.rem(p + k, n_dp), e),
            device_id_type=pl.DeviceIdType.MESH,
        )
    for k in range(1, n_ex):
        pl.semaphore_signal(
            barrier, inc=1, device_id=(p, lax.rem(e + k, n_ex)),
            device_id_type=pl.DeviceIdType.MESH,
        )

    routed = ids_ref[...] == 0
    mask = jnp.max(routed.astype(F32), axis=0, keepdims=True)
    prob = jnp.sum(jnp.where(routed, prob_ref[...], 0.0), axis=0, keepdims=True)
    earlier = (iota((tok, tok), 0) <= iota((tok, tok), 1)).astype(BF)
    place = mm(jnp.broadcast_to(mask, (8, tok)).astype(BF), earlier) - 1.0
    mask_tall = jnp.broadcast_to(mask, (8, tok)) > 0.5
    row = iota((8, tok), 0).astype(F32)
    hit_in = jnp.where((place == row) & (row < CAP) & mask_tall, 1.0, 0.0)
    hit_gr = jnp.where((place + CAP == row) & (row >= CAP) & mask_tall, 1.0, 0.0)
    row_prob = jnp.sum(hit_gr * prob, axis=1, keepdims=True)
    slots = (
        mm(hit_in.astype(BF), li_ref[...]) + row_prob * mm(hit_gr.astype(BF), og_ref[...])
    ).astype(BF)
    for q in range(n_dp):
        slab_out[q] = slots[:, q * depth:(q + 1) * depth]
    pl.semaphore_wait(barrier, n_dp - 1 + n_ex - 1)

    pend = []
    for k in range(1, n_dp):
        q = lax.rem(p + k, n_dp)
        pend.append(send(slab_out.at[q], slabs.at[e, p], s1_send.at[k], s1_recv.at[k], q, e))
    slabs[e, p] = slab_out[p]
    for copy in pend:
        copy.wait()

    pend = [send(slabs.at[e], slabs.at[e], s2_send.at[0], s2_recv.at[0], p, partner)]
    for k in range(1, pairs):
        f = 2 * lax.rem(z + k, pairs) + core
        pend.append(send(slabs.at[e], slabs.at[e], s2_send.at[k], s2_recv.at[k], p, f))

    for copy in w_copies:
        copy.wait()
    tr, tc = depth // TILE, hid // TILE

    def scale_rows(i, carry):
        m, r = i // tr, i % tr
        at = pl.ds(pl.multiple_of(r * TILE, TILE), TILE)
        for j in range(tc):
            power = lax.shift_left(jnp.int32(1), exps_ref[m, r, j] + 15)
            factor = power.astype(F32) * (2.0 ** -15)
            cols = slice(j * TILE, (j + 1) * TILE)
            w[m, at, cols] = (w[m, at, cols].astype(F32) * factor).astype(BF)
        return carry

    lax.fori_loop(0, 3 * tr, scale_rows, 0)

    relays = []
    for k in range(1, pairs):
        pend[k].wait_recv()
        f = 2 * lax.rem(z - k + pairs, pairs) + core
        relays.append(send(slabs.at[f], slabs.at[f], s3_send.at[k], s3_recv.at[k], p, partner))
    pend[0].wait_recv()
    for copy in relays:
        copy.wait_recv()

    src, dst = iota((2 * rows, n_ex * 8), 1), iota((2 * rows, n_ex * 8), 0)
    kind, rest = dst // rows, dst % rows
    pick = jnp.where(
        src == (rest // CAP) * 8 + kind * CAP + rest % CAP, 1.0, 0.0
    ).astype(BF)
    got = [mm(pick, slabs[:, g].reshape(n_ex * 8, depth)) for g in range(n_dp)]
    xs = [
        jnp.concatenate([v[i * rows:(i + 1) * rows] for v in got], axis=0) for i in range(2)
    ]
    for i in range(2):
        x[i] = xs[i].astype(BF)

    sent = []
    for c in range(n_chunk):
        cols = slice(c * chunk, (c + 1) * chunk)
        for m in range(3):
            val = mm(x[m // 2], w[m, :, cols]).astype(F32)
            for g in range(n_dp):
                part_out[c, g, m] = val[g * rows:(g + 1) * rows].astype(BF)
        line = []
        for k in range(1, n_dp):
            q = lax.rem(p + k, n_dp)
            line.append(send(
                part_out.at[c, q], part_in.at[c, k], rs_send.at[c, k], rs_recv.at[c, k], q, e
            ))
        sent.append(line)

    for i in range(2):
        xt_ref[i] = x[i].astype(F32).T.astype(BF)

    shared = []
    for c in range(n_chunk):
        total = [part_out[c, p, m].astype(F32) for m in range(3)]
        for k in range(1, n_dp):
            sent[c][k - 1].wait_recv()
            total = [total[m] + part_in[c, k, m].astype(F32) for m in range(3)]
        gate, up, down = total
        sig = jax.nn.sigmoid(gate)
        act = gate * sig
        acts[c, p, 0] = (down * up * sig * (1.0 + gate * (1.0 - sig))).astype(BF)
        acts[c, p, 1] = (down * act).astype(BF)
        hids[c, p] = (act * up).astype(BF)
        line = []
        for k in range(1, n_dp):
            q = lax.rem(p + k, n_dp)
            line.append(send(
                acts.at[c, p], acts.at[c, p], ag_send.at[c, k], ag_recv.at[c, k], q, e
            ))
        shared.append(line)

    late = []
    for c in range(n_chunk):
        for k in range(1, n_dp):
            q = lax.rem(p + k, n_dp)
            late.append(send(
                hids.at[c, p], hids.at[c, p], hg_send.at[c, k], hg_recv.at[c, k], q, e
            ))

    for c in range(n_chunk):
        cols = slice(c * chunk, (c + 1) * chunk)
        for copy in shared[c]:
            copy.wait_recv()
        full = []
        for m in range(2):
            val = jnp.concatenate(
                [acts[c, g, m].astype(F32) for g in range(n_dp)], axis=0
            ).astype(BF)
            act_ref[m, :, cols] = val
            full.append(val)
        part = mm(full[0], w[0, :, cols], 1, 1) + mm(full[1], w[1, :, cols], 1, 1)
        if c == 0:
            acc[...] = part
        else:
            acc[...] += part

    pad = n_dp * 2
    half = depth // 2
    summed = acc[...].astype(BF)
    batch = min(n_ex, 8)
    for b in range(n_ex // batch):
        shape = (batch * pad, n_dp * rows)
        to, frm = iota(shape, 0), iota(shape, 1)
        f, g = to // pad + b * batch, (to % pad) // 2
        parts = []
        for t in range(CAP):
            piece = CAP * (to % 2) + t
            val = 0.0
            for h in range(2):
                choose = jnp.where(
                    (piece % 2 == h) & (frm == g * rows + f * CAP + piece // 2), 1.0, 0.0
                ).astype(BF)
                val = val + mm(choose, summed[:, h * half:(h + 1) * half])
            parts.append(val)
        val = jnp.concatenate(parts, axis=1)
        for j in range(batch):
            for g in range(n_dp):
                at = j * pad + g * 2
                back_out[b * batch + j, g] = val[at:at + 2].astype(BF)
    back, last = [], []
    if n_dp * n_ex <= DIRECT:
        for kf in range(n_ex - 1, -1, -1):
            for kq in range(n_dp - 1, -1, -1):
                if kq or kf:
                    q, f = lax.rem(p + kq, n_dp), lax.rem(e + kf, n_ex)
                    back.append(send(
                        back_out.at[f, q], back_in.at[e, p],
                        b1_send.at[kf, kq], b1_recv.at[kf, kq], q, f,
                    ))
        back_in[e, p] = back_out[e, p]
        for copy in late:
            copy.wait_recv()
        for c in range(n_chunk):
            act_ref[2, :, c * chunk:(c + 1) * chunk] = jnp.concatenate(
                [hids[c, g].astype(F32) for g in range(n_dp)], axis=0
            ).astype(BF)
        for copy in back:
            copy.wait_recv()
        for q in range(n_dp):
            total = back_in[0, q].astype(F32)
            for f in range(1, n_ex):
                total = total + back_in[f, q].astype(F32)
            own_in[q] = total.astype(BF)
    else:
        for k in range(1, n_ex):
            f = lax.rem(e + k, n_ex)
            back.append(send(back_out.at[f], back_in.at[k], b1_send.at[k, 0], b1_recv.at[k, 0], p, f))
        total = [back_out[e, g].astype(F32) for g in range(n_dp)]
        for k in range(1, n_ex):
            back[k - 1].wait_recv()
            total = [total[g] + back_in[k, g].astype(F32) for g in range(n_dp)]
        for g in range(n_dp):
            own_out[g] = total[g].astype(BF)
        for k in range(1, n_dp):
            q = lax.rem(p + k, n_dp)
            last.append(send(own_out.at[q], own_in.at[p], b2_send.at[k], b2_recv.at[k], q, e))
        own_in[p] = own_out[p]
        for copy in last:
            copy.wait_recv()
        for copy in late:
            copy.wait_recv()
        for c in range(n_chunk):
            act_ref[2, :, c * chunk:(c + 1) * chunk] = jnp.concatenate(
                [hids[c, g].astype(F32) for g in range(n_dp)], axis=0
            ).astype(BF)
    for q in range(n_dp):
        packed = own_in[q].astype(F32)
        halves = [
            packed[j // CAP:j // CAP + 1, (j % CAP) * half:(j % CAP + 1) * half]
            for j in range(2 * CAP)
        ]
        back_rows = jnp.concatenate(
            [jnp.concatenate(halves[2 * c:2 * c + 2], axis=1) for c in range(CAP)], axis=0
        ).astype(BF)
        ig_ref[:, q * depth:(q + 1) * depth] = mm(
            hit_in[:CAP].astype(BF), back_rows, 0, 0
        ).astype(BF)

    for copy in pend[:pairs] + relays + late + back + last:
        copy.wait_send()
    for line in sent + shared:
        for copy in line:
            copy.wait_send()


def grads_kernel(tall, xt_ref, act_ref, out_hbm, out, sems):
    _, depth, hid = out.shape
    steps = depth // tall
    copies = []
    for m in range(3):
        for r in range(steps):
            at = slice(r * tall, (r + 1) * tall)
            out[m, at, :] = mm(xt_ref[m // 2, at, :], act_ref[m])
            copy = pltpu.make_async_copy(
                out.at[m, at], out_hbm.at[m, at], sems.at[m * steps + r]
            )
            copy.start()
            copies.append(copy)
    for copy in copies:
        copy.wait()


def per_device(n_dp, n_ex, out_grad, layer_input, expert_ids, gate_prob, w_stack, scale_exps):
    tok, width = out_grad.shape
    _, depth, hid = w_stack.shape
    rows = n_ex * CAP
    total = n_dp * rows
    chunk = min(256, hid)
    n_chunk = hid // chunk
    n_last = n_dp if n_dp * n_ex <= DIRECT else 1
    vm = pl.BlockSpec(memory_space=pltpu.VMEM)
    dma = pltpu.SemaphoreType.DMA
    pairs = n_ex // 2
    xt, act, input_grad = pl.pallas_call(
        functools.partial(exchange_kernel, n_dp, n_ex, chunk),
        out_shape=(
            jax.ShapeDtypeStruct((2, depth, total), BF),
            jax.ShapeDtypeStruct((3, total, hid), BF),
            jax.ShapeDtypeStruct((tok, width), BF),
        ),
        in_specs=[
            vm, vm, vm, vm,
            pl.BlockSpec(memory_space=pltpu.SMEM),
            pl.BlockSpec(memory_space=pl.ANY),
        ],
        out_specs=(vm, vm, vm),
        scratch_shapes=[
            pltpu.VMEM((3, depth, hid), BF),
            pltpu.VMEM((n_dp, 8, depth), BF),
            pltpu.VMEM((n_ex, n_dp, 8, depth), BF),
            pltpu.VMEM((2, total, depth), BF),
            pltpu.VMEM((n_chunk, n_dp, 3, rows, chunk), BF),
            pltpu.VMEM((n_chunk, n_dp, 3, rows, chunk), BF),
            pltpu.VMEM((n_chunk, n_dp, 2, rows, chunk), BF),
            pltpu.VMEM((n_chunk, n_dp, rows, chunk), BF),
            pltpu.VMEM((total, depth), F32),
            pltpu.VMEM((n_ex, n_dp, 2, CAP * depth // 2), BF),
            pltpu.VMEM((n_ex, n_dp, 2, CAP * depth // 2), BF),
            pltpu.VMEM((n_dp, 2, CAP * depth // 2), BF),
            pltpu.VMEM((n_dp, 2, CAP * depth // 2), BF),
            dma((3,)),
            dma((n_dp,)), dma((n_dp,)),
            dma((pairs,)), dma((pairs,)),
            dma((pairs,)), dma((pairs,)),
            dma((n_chunk, n_dp)), dma((n_chunk, n_dp)),
            dma((n_chunk, n_dp)), dma((n_chunk, n_dp)),
            dma((n_chunk, n_dp)), dma((n_chunk, n_dp)),
            dma((n_ex, n_last)), dma((n_ex, n_last)),
            dma((n_dp,)), dma((n_dp,)),
        ],
        compiler_params=pltpu.CompilerParams(
            collective_id=0, has_side_effects=True, vmem_limit_bytes=VMEM_LIMIT
        ),
    )(out_grad, layer_input, expert_ids.T, gate_prob.T, scale_exps, w_stack)
    tall = min(TALL, depth)
    weight_grads = pl.pallas_call(
        functools.partial(grads_kernel, tall),
        in_specs=[vm, vm],
        out_specs=pl.BlockSpec(memory_space=pl.ANY),
        out_shape=jax.ShapeDtypeStruct((3, depth, hid), F32),
        scratch_shapes=[
            pltpu.VMEM((3, depth, hid), F32),
            dma((3 * (depth // tall),)),
        ],
        compiler_params=pltpu.CompilerParams(vmem_limit_bytes=VMEM_LIMIT),
    )(xt, act)
    return input_grad, weight_grads


def solution(mesh):
    in_specs = (
        P(("dp", "expert"), None),
        P(("dp", "expert"), None),
        P(("dp", "expert"), None),
        P(("dp", "expert"), None),
        P(None, "dp", "expert"),
        P(None, "dp", "expert"),
    )
    out_specs = (P(("dp", "expert"), None), P(None, "dp", "expert"))
    return jax.shard_map(
        functools.partial(per_device, mesh.shape["dp"], mesh.shape["expert"]),
        mesh=mesh, in_specs=in_specs, out_specs=out_specs, check_vma=False,
    )
```

profile of v0, /device:TPU:0, one launch (start us, length us, event | category | flops | bytes accessed | tf_op | source)
XLA Modules:
  0.0 46.4 jit_solution(1074431684281663448)
XLA Ops:
  0.6 40.0 %shard_map.77 = (bf16[2,768,96]{2,1,0:T(8,128)(2,1)}, bf16[3,96,1024]{2,1,0:T(8,128)(2,1)}, bf16[12,3072]{1,0:T(8,128)(2,1)}) custom-call(bf16[12,3072]{1,0:T(8,128)(2,1)} %og_ref.1, bf16[12,3072]{1,0:T(8,128)(2,1)} %li_ref.1, s32[2,12]{1,0:T(2,128)} %bitcast.2, f32[2,12]{1,0:T(2,128)} %bitcast.3, s32[3,6,8]{2,1,0:T(8,128)} %exps_ref.1, ...), custom_call_target="tpu_custom_call" | custom-call | tf_op jit(solution)/shard_map/pallas_call | solution.py:317
  40.6 0.0 copy-start
  40.6 5.2 %shard_map.78 = f32[3,768,1024]{2,1,0:T(8,128)} custom-call(bf16[2,768,96]{2,1,0:T(8,128)(2,1)} %get-tuple-element.6.xt_ref, bf16[3,96,1024]{2,1,0:T(8,128)(2,1)} %get-tuple-element.7.act_ref), custom_call_target="tpu_custom_call" | custom-call | tf_op jit(solution)/shard_map/pallas_call | solution.py:359
  45.8 0.0 copy-done
  45.8 0.6 %copy.9 = bf16[12,3072]{1,0:T(8,128)(2,1)} copy(bf16[12,3072]{1,0:T(8,128)(2,1)S(1)} %copy-done) | data formatting | bytes 147456
Async XLA Ops:
  40.6 5.2 %copy-start = (bf16[12,3072]{1,0:T(8,128)(2,1)S(1)}, bf16[12,3072]{1,0:T(8,128)(2,1)}, u32[]{:S(2)}) copy-start(bf16[12,3072]{1,0:T(8,128)(2,1)} %get-tuple-element.10) | copy-start | bytes 221188
where the time goes:
time: 46.7 us; the launch traced here: 46.4 us
  Pallas kernels  45.1 us (97%)
  between operations  0.66 us (1%)
  local copies, waits for them, and re-layouts  0.65 us (1%)
    pallas_call x1, Pallas kernels, per_device(): pl.pallas_call(functools.partial(exchange_kernel, n_dp, n_ex, chunk), out...  40 us
    pallas_call x1, Pallas kernels, per_device(): pl.pallas_call(functools.partial(grads_kernel, tall), in_specs=[vm, vm],...  5.18 us

commit v1 on v0

--- a/solution.py
+++ b/solution.py
@@ -13,7 +13,7 @@
 TALL = 256
 BF = jnp.bfloat16
 F32 = jnp.float32
-VMEM_LIMIT = 60 * 1024 * 1024
+VMEM_LIMIT = 40 * 1024 * 1024
 
 
 def iota(shape, dim):
@@ -26,14 +26,14 @@
 
 def exchange_kernel(
     n_dp, n_ex, chunk,
-    og_ref, li_ref, ids_ref, prob_ref, exps_ref, w_hbm,
-    xt_ref, act_ref, ig_ref,
-    w, slab_out, slabs, x, part_out, part_in, acts, hids, acc, back_out, back_in, own_out, own_in,
-    w_sem, s1_send, s1_recv, s2_send, s2_recv, s3_send, s3_recv, rs_send, rs_recv,
+    og_hbm, li_hbm, ids_hbm, prob_hbm, exps_hbm, w_hbm,
+    wg_ref, ig_ref,
+    og_ref, li_ref, ids_ref, prob_ref, exps_ref, xt, act, w, slab_out, slabs, x, part_out, part_in, acts, hids, acc, back_out, back_in, own_out, own_in,
+    in_sem, w_sem, s1_send, s1_recv, s2_send, s2_recv, s3_send, s3_recv, rs_send, rs_recv,
     ag_send, ag_recv, hg_send, hg_recv, b1_send, b1_recv, b2_send, b2_recv,
 ):
     p, e = lax.axis_index("dp"), lax.axis_index("expert")
-    tok, width = og_ref.shape
+    tok, width = og_hbm.shape
     _, depth, hid = w.shape
     rows = n_ex * CAP
     n_chunk = hid // chunk
@@ -48,12 +48,6 @@
         )
         copy.start()
         return copy
-
-    w_copies = [
-        pltpu.make_async_copy(w_hbm.at[m], w.at[m], w_sem.at[m]) for m in range(3)
-    ]
-    for copy in w_copies:
-        copy.start()
 
     barrier = pltpu.get_barrier_semaphore()
     for k in range(1, n_dp):
@@ -67,6 +61,23 @@
             device_id_type=pl.DeviceIdType.MESH,
         )
 
+    in_copies = [
+        pltpu.make_async_copy(src, dst, in_sem.at[i])
+        for i, (src, dst) in enumerate((
+            (ids_hbm, ids_ref), (prob_hbm, prob_ref), (li_hbm, li_ref),
+            (og_hbm, og_ref), (exps_hbm, exps_ref),
+        ))
+    ]
+    for copy in in_copies:
+        copy.start()
+    w_copies = [
+        pltpu.make_async_copy(w_hbm.at[m], w.at[m], w_sem.at[m]) for m in range(3)
+    ]
+    for copy in w_copies:
+        copy.start()
+
+    for copy in in_copies[:4]:
+        copy.wait()
     routed = ids_ref[...] == 0
     mask = jnp.max(routed.astype(F32), axis=0, keepdims=True)
     prob = jnp.sum(jnp.where(routed, prob_ref[...], 0.0), axis=0, keepdims=True)
@@ -97,6 +108,7 @@
         f = 2 * lax.rem(z + k, pairs) + core
         pend.append(send(slabs.at[e], slabs.at[e], s2_send.at[k], s2_recv.at[k], p, f))
 
+    in_copies[4].wait()
     for copy in w_copies:
         copy.wait()
     tr, tc = depth // TILE, hid // TILE
@@ -150,7 +162,7 @@
         sent.append(line)
 
     for i in range(2):
-        xt_ref[i] = x[i].astype(F32).T.astype(BF)
+        xt[i] = x[i].astype(F32).T.astype(BF)
 
     shared = []
     for c in range(n_chunk):
@@ -160,10 +172,10 @@
             total = [total[m] + part_in[c, k, m].astype(F32) for m in range(3)]
         gate, up, down = total
         sig = jax.nn.sigmoid(gate)
-        act = gate * sig
+        silu = gate * sig
         acts[c, p, 0] = (down * up * sig * (1.0 + gate * (1.0 - sig))).astype(BF)
-        acts[c, p, 1] = (down * act).astype(BF)
-        hids[c, p] = (act * up).astype(BF)
+        acts[c, p, 1] = (down * silu).astype(BF)
+        hids[c, p] = (silu * up).astype(BF)
         line = []
         for k in range(1, n_dp):
             q = lax.rem(p + k, n_dp)
@@ -189,7 +201,7 @@
             val = jnp.concatenate(
                 [acts[c, g, m].astype(F32) for g in range(n_dp)], axis=0
             ).astype(BF)
-            act_ref[m, :, cols] = val
+            act[m, :, cols] = val
             full.append(val)
         part = mm(full[0], w[0, :, cols], 1, 1) + mm(full[1], w[1, :, cols], 1, 1)
         if c == 0:
@@ -220,6 +232,21 @@
             for g in range(n_dp):
                 at = j * pad + g * 2
                 back_out[b * batch + j, g] = val[at:at + 2].astype(BF)
+    tall = min(TALL, depth)
+
+    def weight_grads():
+        for m in range(3):
+            if m == 2:
+                for copy in late:
+                    copy.wait_recv()
+                for c in range(n_chunk):
+                    act[2, :, c * chunk:(c + 1) * chunk] = jnp.concatenate(
+                        [hids[c, g].astype(F32) for g in range(n_dp)], axis=0
+                    ).astype(BF)
+            for r in range(0, depth, tall):
+                at = slice(r, r + tall)
+                wg_ref[m, at, :] = mm(xt[m // 2, at, :], act[m])
+
     back, last = [], []
     if n_dp * n_ex <= DIRECT:
         for kf in range(n_ex - 1, -1, -1):
@@ -231,12 +258,7 @@
                         b1_send.at[kf, kq], b1_recv.at[kf, kq], q, f,
                     ))
         back_in[e, p] = back_out[e, p]
-        for copy in late:
-            copy.wait_recv()
-        for c in range(n_chunk):
-            act_ref[2, :, c * chunk:(c + 1) * chunk] = jnp.concatenate(
-                [hids[c, g].astype(F32) for g in range(n_dp)], axis=0
-            ).astype(BF)
+        weight_grads()
         for copy in back:
             copy.wait_recv()
         for q in range(n_dp):
@@ -248,6 +270,7 @@
         for k in range(1, n_ex):
             f = lax.rem(e + k, n_ex)
             back.append(send(back_out.at[f], back_in.at[k], b1_send.at[k, 0], b1_recv.at[k, 0], p, f))
+        weight_grads()
         total = [back_out[e, g].astype(F32) for g in range(n_dp)]
         for k in range(1, n_ex):
             back[k - 1].wait_recv()
@@ -260,12 +283,6 @@
         own_in[p] = own_out[p]
         for copy in last:
             copy.wait_recv()
-        for copy in late:
-            copy.wait_recv()
-        for c in range(n_chunk):
-            act_ref[2, :, c * chunk:(c + 1) * chunk] = jnp.concatenate(
-                [hids[c, g].astype(F32) for g in range(n_dp)], axis=0
-            ).astype(BF)
     for q in range(n_dp):
         packed = own_in[q].astype(F32)
         halves = [
@@ -286,19 +303,12 @@
             copy.wait_send()
 
 
-def grads_kernel(tall, xt_ref, act_ref, out_hbm, out, sems):
-    _, depth, hid = out.shape
-    steps = depth // tall
-    copies = []
+def store_kernel(wg_ref, ig_ref, wg_hbm, ig_hbm, sems):
+    copies = [pltpu.make_async_copy(ig_ref, ig_hbm, sems.at[3])]
     for m in range(3):
-        for r in range(steps):
-            at = slice(r * tall, (r + 1) * tall)
-            out[m, at, :] = mm(xt_ref[m // 2, at, :], act_ref[m])
-            copy = pltpu.make_async_copy(
-                out.at[m, at], out_hbm.at[m, at], sems.at[m * steps + r]
-            )
-            copy.start()
-            copies.append(copy)
+        copies.append(pltpu.make_async_copy(wg_ref.at[m], wg_hbm.at[m], sems.at[m]))
+    for copy in copies:
+        copy.start()
     for copy in copies:
         copy.wait()
 
@@ -314,20 +324,22 @@
     vm = pl.BlockSpec(memory_space=pltpu.VMEM)
     dma = pltpu.SemaphoreType.DMA
     pairs = n_ex // 2
-    xt, act, input_grad = pl.pallas_call(
+    weight_grads, input_grad = pl.pallas_call(
         functools.partial(exchange_kernel, n_dp, n_ex, chunk),
         out_shape=(
-            jax.ShapeDtypeStruct((2, depth, total), BF),
-            jax.ShapeDtypeStruct((3, total, hid), BF),
+            jax.ShapeDtypeStruct((3, depth, hid), F32),
             jax.ShapeDtypeStruct((tok, width), BF),
         ),
-        in_specs=[
-            vm, vm, vm, vm,
-            pl.BlockSpec(memory_space=pltpu.SMEM),
-            pl.BlockSpec(memory_space=pl.ANY),
-        ],
-        out_specs=(vm, vm, vm),
+        in_specs=[pl.BlockSpec(memory_space=pltpu.HBM)] * 6,
+        out_specs=(vm, vm),
         scratch_shapes=[
+            pltpu.VMEM((tok, width), BF),
+            pltpu.VMEM((tok, width), BF),
+            pltpu.VMEM((2, tok), jnp.int32),
+            pltpu.VMEM((2, tok), F32),
+            pltpu.SMEM(scale_exps.shape, jnp.int32),
+            pltpu.VMEM((2, depth, total), BF),
+            pltpu.VMEM((3, total, hid), BF),
             pltpu.VMEM((3, depth, hid), BF),
             pltpu.VMEM((n_dp, 8, depth), BF),
             pltpu.VMEM((n_ex, n_dp, 8, depth), BF),
@@ -341,7 +353,7 @@
             pltpu.VMEM((n_ex, n_dp, 2, CAP * depth // 2), BF),
             pltpu.VMEM((n_dp, 2, CAP * depth // 2), BF),
             pltpu.VMEM((n_dp, 2, CAP * depth // 2), BF),
-            dma((3,)),
+            dma((5,)), dma((3,)),
             dma((n_dp,)), dma((n_dp,)),
             dma((pairs,)), dma((pairs,)),
             dma((pairs,)), dma((pairs,)),
@@ -354,19 +366,21 @@
         compiler_params=pltpu.CompilerParams(
             collective_id=0, has_side_effects=True, vmem_limit_bytes=VMEM_LIMIT
         ),
-    )(out_grad, layer_input, expert_ids.T, gate_prob.T, scale_exps, w_stack)
-    tall = min(TALL, depth)
-    weight_grads = pl.pallas_call(
-        functools.partial(grads_kernel, tall),
+    )(*(
+        pltpu.with_memory_space_constraint(v, pltpu.HBM)
+        for v in (out_grad, layer_input, expert_ids.T, gate_prob.T, scale_exps, w_stack)
+    ))
+    weight_grads, input_grad = pl.pallas_call(
+        store_kernel,
         in_specs=[vm, vm],
-        out_specs=pl.BlockSpec(memory_space=pl.ANY),
-        out_shape=jax.ShapeDtypeStruct((3, depth, hid), F32),
-        scratch_shapes=[
-            pltpu.VMEM((3, depth, hid), F32),
-            dma((3 * (depth // tall),)),
-        ],
+        out_specs=(pl.BlockSpec(memory_space=pl.ANY), pl.BlockSpec(memory_space=pl.ANY)),
+        out_shape=(
+            jax.ShapeDtypeStruct((3, depth, hid), F32),
+            jax.ShapeDtypeStruct((tok, width), BF),
+        ),
+        scratch_shapes=[dma((4,))],
         compiler_params=pltpu.CompilerParams(vmem_limit_bytes=VMEM_LIMIT),
-    )(xt, act)
+    )(weight_grads, input_grad)
     return input_grad, weight_grads
 
 

time: 46.7 us -> 42.6 us (0.912)
  Pallas kernels: 45.1 us -> 41.8 us
  local copies, waits for them, and re-layouts: 0.65 us -> 0 us
    pallas_call x1, Pallas kernels: 40 us -> 38 us  [per_device(): pl.pallas_call(functools.partial(exchange_kernel, n_dp, n_ex, chunk), out...]
    pallas_call x1, Pallas kernels: 5.18 us -> 3.8 us  [per_device(): pl.pallas_call(store_kernel, in_specs=[vm, vm], out_specs=(pl.BlockSpec(m...]
    unnamed x3 -> x0, local copies, waits for them, and re-layouts: 0.65 us -> none
where the time goes in v1:
time: 42.6 us; the launch traced here: 42.4 us
  Pallas kernels  41.8 us (98%)
  between operations  0.64 us (2%)
    pallas_call x1, Pallas kernels, per_device(): pl.pallas_call(functools.partial(exchange_kernel, n_dp, n_ex, chunk), out...  38 us
    pallas_call x1, Pallas kernels, per_device(): pl.pallas_call(store_kernel, in_specs=[vm, vm], out_specs=(pl.BlockSpec(m...  3.8 us

profile of v1, /device:TPU:0, one launch (start us, length us, event | category | flops | bytes accessed | tf_op | source)
XLA Modules:
  0.0 42.4 jit_solution(16035835551715300267)
XLA Ops:
  0.6 38.0 %shard_map.77 = (f32[3,768,1024]{2,1,0:T(8,128)S(1)}, bf16[12,3072]{1,0:T(8,128)(2,1)S(1)}) custom-call(bf16[12,3072]{1,0:T(8,128)(2,1)} %og_hbm.1, bf16[12,3072]{1,0:T(8,128)(2,1)} %li_hbm.1, s32[2,12]{1,0:T(2,128)} %bitcast.2, f32[2,12]{1,0:T(2,128)} %bitcast.3, s32[3,6,8]{2,1,0:T(8,128)} %exps_hbm.1, bf16[3,768,1024]{2,1,0:T(8,128)(2,1)} %w_hbm.1), custom_call_target="tpu_custom_call" | custom-call | tf_op jit(solution)/shard_map/pallas_call | solution.py:327
  38.6 3.8 %shard_map.78 = (f32[3,768,1024]{2,1,0:T(8,128)}, bf16[12,3072]{1,0:T(8,128)(2,1)}) custom-call(f32[3,768,1024]{2,1,0:T(8,128)S(1)} %get-tuple-element.6.wg_ref, bf16[12,3072]{1,0:T(8,128)(2,1)S(1)} %get-tuple-element.7.ig_ref), custom_call_target="tpu_custom_call" | custom-call | tf_op jit(solution)/shard_map/pallas_call | solution.py:373

commit v2 on v1

v2 whole, which is shorter than its diff:
```python
import functools

import jax
import jax.numpy as jnp
from jax import lax
from jax.experimental import pallas as pl
from jax.experimental.pallas import tpu as pltpu
from jax.sharding import PartitionSpec as P

TILE = 128
CAP = 3
DIRECT = 64
TALL = 256
BF = jnp.bfloat16
F32 = jnp.float32
VMEM_LIMIT = 40 * 1024 * 1024


def iota(shape, dim):
    return lax.broadcasted_iota(jnp.int32, shape, dim)


def mm(a, b, ca=1, cb=0):
    return lax.dot_general(a, b, (((ca,), (cb,)), ((), ())), preferred_element_type=F32)


def up8(n):
    return -(-n // 8) * 8


def step_to(i, k, n):
    return i ^ k if n & (n - 1) == 0 else lax.rem(i + k, n)


def step_from(i, k, n):
    return i ^ k if n & (n - 1) == 0 else lax.rem(i - k + n, n)


def pad_rows(val, n):
    if val.shape[0] == n:
        return val
    return jnp.concatenate([val, jnp.zeros((n - val.shape[0], val.shape[1]), val.dtype)], axis=0)


class Batch:
    def __init__(self, steps, first, last, n_dp, hid):
        self.steps = steps
        self.rows = len(steps) * 2 * CAP
        self.padded = up8(self.rows)
        tight = up8(3 * self.rows) < 3 * self.padded
        self.stride = self.rows if tight else self.padded
        self.first = first
        self.last = last
        self.all = n_dp * self.padded
        self.mats = 2 if last else 3
        self.sum_rows = up8(3 * self.stride)
        self.act_rows = up8(self.mats * self.stride)
        self.chunk = min(256 if last else 512, hid)
        self.n_chunk = hid // self.chunk

    def cols(self, c):
        return slice(c * self.chunk, (c + 1) * self.chunk)


def plan_batches(n_dp, n_ex, hid):
    pairs = n_ex // 2
    groups = [[0], [1], list(range(2, pairs))] if 2 < pairs <= 4 else [list(range(pairs))]
    batches, first = [], 0
    for i, steps in enumerate(groups):
        batches.append(Batch(steps, first, i == len(groups) - 1, n_dp, hid))
        first += batches[-1].all
    return batches


def exchange_kernel(
    n_dp, n_ex, batches,
    og_hbm, li_hbm, ids_hbm, prob_hbm, exps_hbm, w_hbm,
    wg_ref, ig_ref, *scratch,
):
    n_b = len(batches)
    (
        og_ref, li_ref, ids_ref, prob_ref, exps_ref, xt, act, w, slab_out, slabs, x, hid_out, hid_in,
        acc, back_out, back_in, own_out, own_in,
        in_sem, s1_send, s1_recv, s2_send, s2_recv, s3_send, s3_recv, ready,
        rs_send, rs_recv, ag_send, ag_recv, hg_sem, b1_sem, b2_sem,
    ) = scratch[:33]
    bufs = scratch[33:]
    part_out, part_in, act_out, act_in = (bufs[i * n_b:(i + 1) * n_b] for i in range(4))
    p, e = lax.axis_index("dp"), lax.axis_index("expert")
    tok, width = og_hbm.shape
    _, depth, hid = w.shape
    pairs = n_ex // 2
    z, core = e // 2, e % 2
    other = 1 - core
    partner = 2 * z + other

    def send(src, dst, ssem, rsem, q, f):
        pltpu.make_async_remote_copy(
            src_ref=src, dst_ref=dst, send_sem=ssem, recv_sem=rsem,
            device_id=(q, f), device_id_type=pl.DeviceIdType.MESH,
        ).start()

    def wait(ref, sem):
        pltpu.make_async_copy(ref, ref, sem).wait()

    def tell(sem, q, f):
        pl.semaphore_signal(sem, inc=1, device_id=(q, f), device_id_type=pl.DeviceIdType.MESH)

    in_copies = [
        pltpu.make_async_copy(src, dst, in_sem.at[i])
        for i, (src, dst) in enumerate((
            (ids_hbm, ids_ref), (prob_hbm, prob_ref), (li_hbm, li_ref),
            (og_hbm, og_ref), (exps_hbm, exps_ref), (w_hbm, w),
        ))
    ]
    for copy in in_copies[:5]:
        copy.start()

    barrier = pltpu.get_barrier_semaphore()
    for k in range(1, n_dp):
        tell(barrier, step_from(p, k, n_dp), partner)
    tell(barrier, p, partner)
    for j in range(1, pairs):
        s = step_from(z, j, pairs)

        @pl.when(s > z)
        def _(s=s):
            tell(barrier, p, 2 * s + other)

    for copy in in_copies[:4]:
        copy.wait()
    in_copies[5].start()
    routed = ids_ref[...] == 0
    mask = jnp.max(routed.astype(F32), axis=0, keepdims=True)
    prob = jnp.sum(jnp.where(routed, prob_ref[...], 0.0), axis=0, keepdims=True)
    earlier = (iota((tok, tok), 0) <= iota((tok, tok), 1)).astype(BF)
    place = mm(jnp.broadcast_to(mask, (8, tok)).astype(BF), earlier) - 1.0
    mask_tall = jnp.broadcast_to(mask, (8, tok)) > 0.5
    row = iota((8, tok), 0).astype(F32)
    hit_in = jnp.where((place == row) & (row < CAP) & mask_tall, 1.0, 0.0)
    hit_gr = jnp.where((place + CAP == row) & (row >= CAP) & mask_tall, 1.0, 0.0)
    row_prob = jnp.sum(hit_gr * prob, axis=1, keepdims=True)
    slots = (
        mm(hit_in.astype(BF), li_ref[...]) + row_prob * mm(hit_gr.astype(BF), og_ref[...])
    ).astype(BF)
    for q in range(n_dp):
        slab_out[q] = slots[:, q * depth:(q + 1) * depth]
    pl.semaphore_wait(barrier, n_dp + z)

    for k in range(n_dp - 1, 0, -1):
        q = step_to(p, k, n_dp)
        send(slab_out.at[q], slabs.at[z, other, p], s1_send, s1_recv.at[k], q, partner)
    for j in range(1, pairs):
        s = step_from(z, j, pairs)

        @pl.when(s < z)
        def _(s=s, j=j):
            tell(ready.at[j], p, 2 * s + other)

    slabs[z, core, p] = slab_out[p]

    def forward_down(src):
        for j in range(pairs - 1, 0, -1):
            t = step_to(z, j, pairs)

            @pl.when(t < z)
            def _(t=t, j=j):
                send(src, src, s2_send, s2_recv.at[j], p, 2 * t + other)

    fine = n_dp <= 4
    if fine:
        forward_down(slabs.at[z, core, p])

    in_copies[4].wait()
    in_copies[5].wait()
    tr, tc = depth // TILE, hid // TILE

    def scale_rows(i, carry):
        m, r = i // tr, i % tr
        at = pl.ds(pl.multiple_of(r * TILE, TILE), TILE)
        for j in range(tc):
            power = lax.shift_left(jnp.int32(1), exps_ref[m, r, j] + 15)
            factor = power.astype(F32) * (2.0 ** -15)
            cols = slice(j * TILE, (j + 1) * TILE)
            w[m, at, cols] = (w[m, at, cols].astype(F32) * factor).astype(BF)
        return carry

    lax.fori_loop(0, 3 * tr, scale_rows, 0)

    for k in range(1, n_dp):
        q = step_from(p, k, n_dp)
        wait(slabs.at[z, core, q], s1_recv.at[k])
        if fine:
            forward_down(slabs.at[z, core, q])
    held = slabs.at[z, core]
    send(held, held, s3_send, s3_recv.at[0], p, partner)
    if not fine:
        forward_down(held)
    for j in range(1, pairs):
        t = step_to(z, j, pairs)

        @pl.when(t > z)
        def _(t=t, j=j):
            pl.semaphore_wait(ready.at[j], 1)
            send(held, held, s2_send, s2_recv.at[j], p, 2 * t + other)

    def pass_on(b):
        for j in b.steps:
            if j:
                block = slabs.at[step_from(z, j, pairs), other]
                wait(block, s2_recv.at[j])
                send(block, block, s3_send, s3_recv.at[j], p, partner)

    def collect(b):
        for j in b.steps:
            s = step_from(z, j, pairs)
            wait(slabs.at[s, core if j else other], s3_recv.at[j])
        shape = (2 * b.padded, len(b.steps) * 16)
        src, dst = iota(shape, 1), iota(shape, 0)
        kind, r = dst // b.padded, dst % b.padded
        jl, cs, c = r // (2 * CAP), (r // CAP) % 2, r % CAP
        rows = [[], []]
        for g in range(n_dp):
            h = jnp.where(g == p, cs, 1 - cs)
            pick = jnp.where(
                (src == jl * 16 + h * 8 + kind * CAP + c) & (r < b.rows), 1.0, 0.0
            ).astype(BF)
            have = jnp.concatenate(
                [slabs[step_from(z, j, pairs), :, g].reshape(16, depth) for j in b.steps], axis=0
            )
            val = mm(pick, have)
            for i in range(2):
                rows[i].append(val[i * b.padded:(i + 1) * b.padded])
        for i in range(2):
            x[i, b.first:b.first + b.all] = jnp.concatenate(rows[i], axis=0).astype(BF)

    def multiply(n, c):
        b = batches[n]
        vals = [
            mm(x[m // 2, b.first:b.first + b.all], w[m, :, b.cols(c)]) for m in range(3)
        ]
        for g in range(n_dp):
            at = g * b.padded
            block = jnp.concatenate([v[at:at + b.stride] for v in vals], axis=0)
            part_out[n][c, g] = pad_rows(block, b.sum_rows).astype(BF)
        for k in range(n_dp - 1, -1, -1):
            q = step_to(p, k, n_dp)
            send(part_out[n].at[c, q], part_in[n].at[c, p], rs_send.at[n], rs_recv.at[n, c], q, partner)

    pass_on(batches[0])
    for n, b in enumerate(batches):
        collect(b)
        for c in range(b.n_chunk):
            if c == b.n_chunk - 1 and not b.last:
                if c == 0 or n > 0:
                    pass_on(batches[n + 1])
            multiply(n, c)
        if n == 0 and b.n_chunk > 1 and not b.last:
            pass_on(batches[1])

    for i in range(2):
        xt[i] = x[i].astype(F32).T.astype(BF)

    for n, b in enumerate(batches):
        for c in range(b.n_chunk):
            wait(part_in[n].at[c], rs_recv.at[n, c])
            total = part_in[n][c, 0].astype(F32)
            for g in range(1, n_dp):
                total = total + part_in[n][c, g].astype(F32)
            gate, up, down = (total[m * b.stride:(m + 1) * b.stride] for m in range(3))
            sig = jax.nn.sigmoid(gate)
            silu = gate * sig
            grads = [down * up * sig * (1.0 + gate * (1.0 - sig)), down * silu]
            hidden = silu * up
            if b.last:
                hid_out[:, b.cols(c)] = pad_rows(hidden, b.padded).astype(BF)
            else:
                grads.append(hidden)
            act_out[n][c] = pad_rows(jnp.concatenate(grads, axis=0), b.act_rows).astype(BF)
            for k in range(n_dp - 1, -1, -1):
                q = step_to(p, k, n_dp)
                send(act_out[n].at[c], act_in[n].at[c, p], ag_send.at[n], ag_recv.at[n, c], q, partner)
    for k in range(n_dp - 1, -1, -1):
        send(hid_out, hid_in.at[p], hg_sem.at[0], hg_sem.at[1], step_to(p, k, n_dp), partner)

    def unpack(n, c):
        b = batches[n]
        wait(act_in[n].at[c], ag_recv.at[n, c])
        blocks = [act_in[n][c, g].astype(F32) for g in range(n_dp)]
        for m in range(b.mats):
            val = [pad_rows(v[m * b.stride:(m + 1) * b.stride], b.padded) for v in blocks]
            act[m, b.first:b.first + b.all, b.cols(c)] = jnp.concatenate(val, axis=0).astype(BF)

    for n, b in enumerate(batches):
        for c in range(b.n_chunk):
            unpack(n, c)
            if b.last:
                cols = b.cols(c)
                part = mm(act[0, :, cols], w[0, :, cols], 1, 1) + mm(act[1, :, cols], w[1, :, cols], 1, 1)
                if c == 0:
                    acc[...] = part
                else:
                    acc[...] += part

    pad = n_dp * 2
    half = depth // 2
    summed = acc[...].astype(BF)
    some = min(n_ex, 8)
    for i in range(n_ex // some):
        shape = (some * pad, summed.shape[0])
        to, frm = iota(shape, 0), iota(shape, 1)
        f, g = to // pad + i * some, (to % pad) // 2
        cs = jnp.where(core == 0, f % 2, 1 - f % 2)
        if n_b == 1:
            base = g * batches[0].padded + (f // 2) * 2 * CAP
        else:
            base = 0
            for b in batches:
                for jl, j in enumerate(b.steps):
                    base = jnp.where(f // 2 == j, b.first + g * b.padded + jl * 2 * CAP, base)
        base = base + cs * CAP
        parts = []
        for t in range(CAP):
            piece = CAP * (to % 2) + t
            val = 0.0
            for h in range(2):
                choose = jnp.where(
                    (piece % 2 == h) & (frm == base + piece // 2), 1.0, 0.0
                ).astype(BF)
                val = val + mm(choose, summed[:, h * half:(h + 1) * half])
            parts.append(val)
        val = jnp.concatenate(parts, axis=1)
        for j in range(some):
            for g in range(n_dp):
                at = j * pad + g * 2
                back_out[i * some + j, g] = val[at:at + 2].astype(BF)

    tall = min(TALL, depth)

    def weight_grads():
        for m in range(3):
            if m == 2:
                b = batches[-1]
                wait(hid_in, hg_sem.at[1])
                act[2, b.first:b.first + b.all] = jnp.concatenate(
                    [hid_in[g].astype(F32) for g in range(n_dp)], axis=0
                ).astype(BF)
            for r in range(0, depth, tall):
                at = slice(r, r + tall)
                wg_ref[m, at, :] = mm(xt[m // 2, at, :], act[m])

    def place(q, packed):
        halves = [
            packed[j // CAP:j // CAP + 1, (j % CAP) * half:(j % CAP + 1) * half]
            for j in range(2 * CAP)
        ]
        back_rows = jnp.concatenate(
            [jnp.concatenate(halves[2 * c:2 * c + 2], axis=1) for c in range(CAP)], axis=0
        ).astype(BF)
        ig_ref[:, pl.ds(pl.multiple_of(q * depth, TILE), depth)] = mm(
            hit_in[:CAP].astype(BF), back_rows, 0, 0
        ).astype(BF)

    def far(k):
        return 2 * step_to(z, k // 2, pairs) + (core ^ (k % 2))

    if n_dp * n_ex <= DIRECT:
        for r in range(n_ex * n_dp - 1, 0, -1):
            q = step_to(p, r % n_dp, n_dp)
            send(
                back_out.at[r // n_dp, q], back_in.at[r], b1_sem.at[0], b1_sem.at[1],
                q, far(r // n_dp),
            )
        back_in[0] = back_out[0, p]
        weight_grads()
        arrived = back_in.at[1:n_ex * n_dp]
        wait(arrived, b1_sem.at[1])
        for k in range(n_dp):
            total = back_in[k].astype(F32)
            for f in range(1, n_ex):
                total = total + back_in[f * n_dp + k].astype(F32)
            place(step_from(p, k, n_dp), total)
        wait(arrived, b1_sem.at[0])
    else:
        for k in range(1, n_ex):
            send(back_out.at[k], back_in.at[k], b1_sem.at[0], b1_sem.at[1], p, far(k))
        weight_grads()
        arrived = back_in.at[1:n_ex]
        wait(arrived, b1_sem.at[1])
        for g in range(n_dp):
            total = back_out[0, g].astype(F32)
            for k in range(1, n_ex):
                total = total + back_in[k, g].astype(F32)
            own_out[g] = total.astype(BF)
        for k in range(1, n_dp):
            q = step_to(p, k, n_dp)
            send(own_out.at[q], own_in.at[k], b2_sem.at[0], b2_sem.at[1], q, e)
        own_in[0] = own_out[p]
        landed = own_in.at[1:n_dp]
        wait(landed, b2_sem.at[1])
        for k in range(n_dp):
            place(step_from(p, k, n_dp), own_in[k].astype(F32))
        wait(arrived, b1_sem.at[0])
        wait(landed, b2_sem.at[0])

    wait(slab_out.at[1:n_dp], s1_send)
    wait(slabs.at[1:pairs, 0], s2_send)
    wait(slabs.at[:, 0], s3_send)
    for n in range(n_b):
        wait(part_out[n], rs_send.at[n])
        wait(act_in[n], ag_send.at[n])
    wait(hid_in, hg_sem.at[0])


def store_kernel(wg_ref, ig_ref, wg_hbm, ig_hbm, sems):
    copies = [pltpu.make_async_copy(ig_ref, ig_hbm, sems.at[3])]
    for m in range(3):
        copies.append(pltpu.make_async_copy(wg_ref.at[m], wg_hbm.at[m], sems.at[m]))
    for copy in copies:
        copy.start()
    for copy in copies:
        copy.wait()


def per_device(n_dp, n_ex, out_grad, layer_input, expert_ids, gate_prob, w_stack, scale_exps):
    tok, width = out_grad.shape
    _, depth, hid = w_stack.shape
    batches = plan_batches(n_dp, n_ex, hid)
    total = sum(b.all for b in batches)
    n_b = len(batches)
    most = max(b.n_chunk for b in batches)
    pairs = n_ex // 2
    packed = (2, CAP * depth // 2)
    direct = n_dp * n_ex <= DIRECT
    vm = pl.BlockSpec(memory_space=pltpu.VMEM)
    dma = pltpu.SemaphoreType.DMA
    weight_grads, input_grad = pl.pallas_call(
        functools.partial(exchange_kernel, n_dp, n_ex, batches),
        out_shape=(
            jax.ShapeDtypeStruct((3, depth, hid), F32),
            jax.ShapeDtypeStruct((tok, width), BF),
        ),
        in_specs=[pl.BlockSpec(memory_space=pltpu.HBM)] * 6,
        out_specs=(vm, vm),
        scratch_shapes=[
            pltpu.VMEM((tok, width), BF),
            pltpu.VMEM((tok, width), BF),
            pltpu.VMEM((2, tok), jnp.int32),
            pltpu.VMEM((2, tok), F32),
            pltpu.SMEM(scale_exps.shape, jnp.int32),
            pltpu.VMEM((2, depth, total), BF),
            pltpu.VMEM((3, total, hid), BF),
            pltpu.VMEM((3, depth, hid), BF),
            pltpu.VMEM((n_dp, 8, depth), BF),
            pltpu.VMEM((pairs, 2, n_dp, 8, depth), BF),
            pltpu.VMEM((2, total, depth), BF),
            pltpu.VMEM((batches[-1].padded, hid), BF),
            pltpu.VMEM((n_dp, batches[-1].padded, hid), BF),
            pltpu.VMEM((total, depth), F32),
            pltpu.VMEM((n_ex, n_dp) + packed, BF),
            pltpu.VMEM(((n_ex * n_dp,) if direct else (n_ex, n_dp)) + packed, BF),
            pltpu.VMEM((n_dp,) + packed, BF),
            pltpu.VMEM((n_dp,) + packed, BF),
            dma((6,)),
            dma, dma((n_dp,)),
            dma, dma((pairs,)),
            dma, dma((pairs,)),
            pltpu.SemaphoreType.REGULAR((pairs,)),
            dma((n_b,)), dma((n_b, most)),
            dma((n_b,)), dma((n_b, most)),
            dma((2,)), dma((2,)), dma((2,)),
        ]
        + [pltpu.VMEM((b.n_chunk, n_dp, b.sum_rows, b.chunk), BF) for b in batches]
        + [pltpu.VMEM((b.n_chunk, n_dp, b.sum_rows, b.chunk), BF) for b in batches]
        + [pltpu.VMEM((b.n_chunk, b.act_rows, b.chunk), BF) for b in batches]
        + [pltpu.VMEM((b.n_chunk, n_dp, b.act_rows, b.chunk), BF) for b in batches],
        compiler_params=pltpu.CompilerParams(
            collective_id=0, has_side_effects=True, vmem_limit_bytes=VMEM_LIMIT
        ),
    )(*(
        pltpu.with_memory_space_constraint(v, pltpu.HBM)
        for v in (out_grad, layer_input, expert_ids.T, gate_prob.T, scale_exps, w_stack)
    ))
    weight_grads, input_grad = pl.pallas_call(
        store_kernel,
        in_specs=[vm, vm],
        out_specs=(pl.BlockSpec(memory_space=pl.ANY), pl.BlockSpec(memory_space=pl.ANY)),
        out_shape=(
            jax.ShapeDtypeStruct((3, depth, hid), F32),
            jax.ShapeDtypeStruct((tok, width), BF),
        ),
        scratch_shapes=[dma((4,))],
        compiler_params=pltpu.CompilerParams(vmem_limit_bytes=VMEM_LIMIT),
    )(weight_grads, input_grad)
    return input_grad, weight_grads


def solution(mesh):
    in_specs = (
        P(("dp", "expert"), None),
        P(("dp", "expert"), None),
        P(("dp", "expert"), None),
        P(("dp", "expert"), None),
        P(None, "dp", "expert"),
        P(None, "dp", "expert"),
    )
    out_specs = (P(("dp", "expert"), None), P(None, "dp", "expert"))
    return jax.shard_map(
        functools.partial(per_device, mesh.shape["dp"], mesh.shape["expert"]),
        mesh=mesh, in_specs=in_specs, out_specs=out_specs, check_vma=False,
    )
```

time: 42.6 us -> 40.1 us (0.941)
  Pallas kernels: 41.8 us -> 39.3 us
    pallas_call x1, Pallas kernels: 38 us -> 35.5 us  [per_device(): pl.pallas_call(functools.partial(exchange_kernel, n_dp, n_ex, batches), o...]
where the time goes in v2:
time: 40.1 us; the launch traced here: 40 us
  Pallas kernels  39.3 us (98%)
  between operations  0.64 us (2%)
    pallas_call x1, Pallas kernels, per_device(): pl.pallas_call(functools.partial(exchange_kernel, n_dp, n_ex, batches), o...  35.5 us
    pallas_call x1, Pallas kernels, per_device(): pl.pallas_call(store_kernel, in_specs=[vm, vm], out_specs=(pl.BlockSpec(m...  3.8 us

profile of v2, /device:TPU:0, one launch (start us, length us, event | category | flops | bytes accessed | tf_op | source)
XLA Modules:
  0.0 40.0 jit_solution(14607526987080858136)
XLA Ops:
  0.6 35.5 %shard_map.77 = (f32[3,768,1024]{2,1,0:T(8,128)S(1)}, bf16[12,3072]{1,0:T(8,128)(2,1)S(1)}) custom-call(bf16[12,3072]{1,0:T(8,128)(2,1)} %og_hbm.1, bf16[12,3072]{1,0:T(8,128)(2,1)} %li_hbm.1, s32[2,12]{1,0:T(2,128)} %bitcast.2, f32[2,12]{1,0:T(2,128)} %bitcast.3, s32[3,6,8]{2,1,0:T(8,128)} %exps_hbm.1, bf16[3,768,1024]{2,1,0:T(8,128)(2,1)} %w_hbm.1), custom_call_target="tpu_custom_call" | custom-call | tf_op jit(solution)/shard_map/pallas_call | solution.py:437
  36.2 3.8 %shard_map.78 = (f32[3,768,1024]{2,1,0:T(8,128)}, bf16[12,3072]{1,0:T(8,128)(2,1)}) custom-call(f32[3,768,1024]{2,1,0:T(8,128)S(1)} %get-tuple-element.6.wg_ref, bf16[12,3072]{1,0:T(8,128)(2,1)S(1)} %get-tuple-element.7.ig_ref), custom_call_target="tpu_custom_call" | custom-call | tf_op jit(solution)/shard_map/pallas_call | solution.py:484

commit v3 on v2

--- a/solution.py
+++ b/solution.py
@@ -52,10 +52,10 @@
         self.first = first
         self.last = last
         self.all = n_dp * self.padded
-        self.mats = 2 if last else 3
+        self.local = first // n_dp
         self.sum_rows = up8(3 * self.stride)
-        self.act_rows = up8(self.mats * self.stride)
-        self.chunk = min(256 if last else 512, hid)
+        self.act_rows = up8(2 * self.stride)
+        self.chunk = min(128, hid) if last else hid
         self.n_chunk = hid // self.chunk
 
     def cols(self, c):
@@ -64,11 +64,12 @@
 
 def plan_batches(n_dp, n_ex, hid):
     pairs = n_ex // 2
-    groups = [[0], [1], list(range(2, pairs))] if 2 < pairs <= 4 else [list(range(pairs))]
+    groups = [[0], list(range(1, pairs))] if 1 < pairs <= 4 else [list(range(pairs))]
     batches, first = [], 0
     for i, steps in enumerate(groups):
         batches.append(Batch(steps, first, i == len(groups) - 1, n_dp, hid))
         first += batches[-1].all
+        batches[-1].slot = sum(b.n_chunk for b in batches[:-1])
     return batches
 
 
@@ -110,7 +111,8 @@
         pltpu.make_async_copy(src, dst, in_sem.at[i])
         for i, (src, dst) in enumerate((
             (ids_hbm, ids_ref), (prob_hbm, prob_ref), (li_hbm, li_ref),
-            (og_hbm, og_ref), (exps_hbm, exps_ref), (w_hbm, w),
+            (og_hbm, og_ref), (exps_hbm, exps_ref),
+            (w_hbm.at[0], w.at[0]), (w_hbm.at[1], w.at[1]), (w_hbm.at[2], w.at[2]),
         ))
     ]
     for copy in in_copies[:5]:
@@ -129,7 +131,8 @@
 
     for copy in in_copies[:4]:
         copy.wait()
-    in_copies[5].start()
+    for copy in in_copies[5:]:
+        copy.start()
     routed = ids_ref[...] == 0
     mask = jnp.max(routed.astype(F32), axis=0, keepdims=True)
     prob = jnp.sum(jnp.where(routed, prob_ref[...], 0.0), axis=0, keepdims=True)
@@ -172,11 +175,9 @@
         forward_down(slabs.at[z, core, p])
 
     in_copies[4].wait()
-    in_copies[5].wait()
     tr, tc = depth // TILE, hid // TILE
 
-    def scale_rows(i, carry):
-        m, r = i // tr, i % tr
+    def scale_rows(m, r, carry):
         at = pl.ds(pl.multiple_of(r * TILE, TILE), TILE)
         for j in range(tc):
             power = lax.shift_left(jnp.int32(1), exps_ref[m, r, j] + 15)
@@ -185,7 +186,9 @@
             w[m, at, cols] = (w[m, at, cols].astype(F32) * factor).astype(BF)
         return carry
 
-    lax.fori_loop(0, 3 * tr, scale_rows, 0)
+    for m in range(3):
+        in_copies[5 + m].wait()
+        lax.fori_loop(0, tr, functools.partial(scale_rows, m), 0)
 
     for k in range(1, n_dp):
         q = step_from(p, k, n_dp)
@@ -245,49 +248,52 @@
             part_out[n][c, g] = pad_rows(block, b.sum_rows).astype(BF)
         for k in range(n_dp - 1, -1, -1):
             q = step_to(p, k, n_dp)
-            send(part_out[n].at[c, q], part_in[n].at[c, p], rs_send.at[n], rs_recv.at[n, c], q, partner)
-
-    pass_on(batches[0])
-    for n, b in enumerate(batches):
-        collect(b)
-        for c in range(b.n_chunk):
-            if c == b.n_chunk - 1 and not b.last:
-                if c == 0 or n > 0:
-                    pass_on(batches[n + 1])
-            multiply(n, c)
-        if n == 0 and b.n_chunk > 1 and not b.last:
-            pass_on(batches[1])
+            send(part_out[n].at[c, q], part_in[n].at[c, p], rs_send.at[n], rs_recv.at[b.slot + c], q, partner)
+
+    def activate(n, c):
+        b = batches[n]
+        wait(part_in[n].at[c], rs_recv.at[b.slot + c])
+        total = part_in[n][c, 0].astype(F32)
+        for g in range(1, n_dp):
+            total = total + part_in[n][c, g].astype(F32)
+        gate, up, down = (total[m * b.stride:(m + 1) * b.stride] for m in range(3))
+        sig = jax.nn.sigmoid(gate)
+        silu = gate * sig
+        grads = [down * up * sig * (1.0 + gate * (1.0 - sig)), down * silu]
+        hid_out[b.local:b.local + b.padded, b.cols(c)] = pad_rows(silu * up, b.padded).astype(BF)
+        act_out[n][c] = pad_rows(jnp.concatenate(grads, axis=0), b.act_rows).astype(BF)
+        for k in range(n_dp - 1, -1, -1):
+            q = step_to(p, k, n_dp)
+            send(
+                act_out[n].at[c], act_in[n].at[c, p], ag_send.at[n], ag_recv.at[b.slot + c],
+                q, partner,
+            )
+
+    if n_b == 1:
+        pass_on(batches[0])
+    collect(batches[0])
+    if n_b > 1:
+        multiply(0, 0)
+        pass_on(batches[1])
+        activate(0, 0)
+        collect(batches[1])
+    for c in range(batches[-1].n_chunk):
+        multiply(n_b - 1, c)
 
     for i in range(2):
         xt[i] = x[i].astype(F32).T.astype(BF)
 
-    for n, b in enumerate(batches):
+    for n, b in list(enumerate(batches))[-1:]:
         for c in range(b.n_chunk):
-            wait(part_in[n].at[c], rs_recv.at[n, c])
-            total = part_in[n][c, 0].astype(F32)
-            for g in range(1, n_dp):
-                total = total + part_in[n][c, g].astype(F32)
-            gate, up, down = (total[m * b.stride:(m + 1) * b.stride] for m in range(3))
-            sig = jax.nn.sigmoid(gate)
-            silu = gate * sig
-            grads = [down * up * sig * (1.0 + gate * (1.0 - sig)), down * silu]
-            hidden = silu * up
-            if b.last:
-                hid_out[:, b.cols(c)] = pad_rows(hidden, b.padded).astype(BF)
-            else:
-                grads.append(hidden)
-            act_out[n][c] = pad_rows(jnp.concatenate(grads, axis=0), b.act_rows).astype(BF)
-            for k in range(n_dp - 1, -1, -1):
-                q = step_to(p, k, n_dp)
-                send(act_out[n].at[c], act_in[n].at[c, p], ag_send.at[n], ag_recv.at[n, c], q, partner)
+            activate(n, c)
     for k in range(n_dp - 1, -1, -1):
         send(hid_out, hid_in.at[p], hg_sem.at[0], hg_sem.at[1], step_to(p, k, n_dp), partner)
 
     def unpack(n, c):
         b = batches[n]
-        wait(act_in[n].at[c], ag_recv.at[n, c])
+        wait(act_in[n].at[c], ag_recv.at[b.slot + c])
         blocks = [act_in[n][c, g].astype(F32) for g in range(n_dp)]
-        for m in range(b.mats):
+        for m in range(2):
             val = [pad_rows(v[m * b.stride:(m + 1) * b.stride], b.padded) for v in blocks]
             act[m, b.first:b.first + b.all, b.cols(c)] = jnp.concatenate(val, axis=0).astype(BF)
 
@@ -340,11 +346,12 @@
     def weight_grads():
         for m in range(3):
             if m == 2:
-                b = batches[-1]
                 wait(hid_in, hg_sem.at[1])
-                act[2, b.first:b.first + b.all] = jnp.concatenate(
-                    [hid_in[g].astype(F32) for g in range(n_dp)], axis=0
-                ).astype(BF)
+                for b in batches:
+                    act[2, b.first:b.first + b.all] = jnp.concatenate(
+                        [hid_in[g, b.local:b.local + b.padded].astype(F32) for g in range(n_dp)],
+                        axis=0,
+                    ).astype(BF)
             for r in range(0, depth, tall):
                 at = slice(r, r + tall)
                 wg_ref[m, at, :] = mm(xt[m // 2, at, :], act[m])
@@ -428,7 +435,7 @@
     batches = plan_batches(n_dp, n_ex, hid)
     total = sum(b.all for b in batches)
     n_b = len(batches)
-    most = max(b.n_chunk for b in batches)
+    parts = sum(b.n_chunk for b in batches)
     pairs = n_ex // 2
     packed = (2, CAP * depth // 2)
     direct = n_dp * n_ex <= DIRECT
@@ -454,20 +461,20 @@
             pltpu.VMEM((n_dp, 8, depth), BF),
             pltpu.VMEM((pairs, 2, n_dp, 8, depth), BF),
             pltpu.VMEM((2, total, depth), BF),
-            pltpu.VMEM((batches[-1].padded, hid), BF),
-            pltpu.VMEM((n_dp, batches[-1].padded, hid), BF),
+            pltpu.VMEM((total // n_dp, hid), BF),
+            pltpu.VMEM((n_dp, total // n_dp, hid), BF),
             pltpu.VMEM((total, depth), F32),
             pltpu.VMEM((n_ex, n_dp) + packed, BF),
             pltpu.VMEM(((n_ex * n_dp,) if direct else (n_ex, n_dp)) + packed, BF),
             pltpu.VMEM((n_dp,) + packed, BF),
             pltpu.VMEM((n_dp,) + packed, BF),
-            dma((6,)),
+            dma((8,)),
             dma, dma((n_dp,)),
             dma, dma((pairs,)),
             dma, dma((pairs,)),
             pltpu.SemaphoreType.REGULAR((pairs,)),
-            dma((n_b,)), dma((n_b, most)),
-            dma((n_b,)), dma((n_b, most)),
+            dma((n_b,)), dma((parts,)),
+            dma((n_b,)), dma((parts,)),
             dma((2,)), dma((2,)), dma((2,)),
         ]
         + [pltpu.VMEM((b.n_chunk, n_dp, b.sum_rows, b.chunk), BF) for b in batches]

time: 40.1 us -> 37.5 us (0.935)
  Pallas kernels: 39.3 us -> 36.6 us
    pallas_call x1, Pallas kernels: 35.5 us -> 32.7 us  [per_device(): pl.pallas_call(functools.partial(exchange_kernel, n_dp, n_ex, batches), o...]
where the time goes in v3:
time: 37.5 us; the launch traced here: 37.2 us
  Pallas kernels  36.6 us (98%)
  between operations  0.64 us (2%)
    pallas_call x1, Pallas kernels, per_device(): pl.pallas_call(functools.partial(exchange_kernel, n_dp, n_ex, batches), o...  32.7 us
    pallas_call x1, Pallas kernels, per_device(): pl.pallas_call(store_kernel, in_specs=[vm, vm], out_specs=(pl.BlockSpec(m...  3.8 us

profile of v3, /device:TPU:0, one launch (start us, length us, event | category | flops | bytes accessed | tf_op | source)
XLA Modules:
  0.0 37.2 jit_solution(3938481430544350092)
XLA Ops:
  0.6 32.7 %shard_map.77 = (f32[3,768,1024]{2,1,0:T(8,128)S(1)}, bf16[12,3072]{1,0:T(8,128)(2,1)S(1)}) custom-call(bf16[12,3072]{1,0:T(8,128)(2,1)} %og_hbm.1, bf16[12,3072]{1,0:T(8,128)(2,1)} %li_hbm.1, s32[2,12]{1,0:T(2,128)} %bitcast.2, f32[2,12]{1,0:T(2,128)} %bitcast.3, s32[3,6,8]{2,1,0:T(8,128)} %exps_hbm.1, bf16[3,768,1024]{2,1,0:T(8,128)(2,1)} %w_hbm.1), custom_call_target="tpu_custom_call" | custom-call | tf_op jit(solution)/shard_map/pallas_call | solution.py:444
  33.4 3.8 %shard_map.78 = (f32[3,768,1024]{2,1,0:T(8,128)}, bf16[12,3072]{1,0:T(8,128)(2,1)}) custom-call(f32[3,768,1024]{2,1,0:T(8,128)S(1)} %get-tuple-element.6.wg_ref, bf16[12,3072]{1,0:T(8,128)(2,1)S(1)} %get-tuple-element.7.ig_ref), custom_call_target="tpu_custom_call" | custom-call | tf_op jit(solution)/shard_map/pallas_call | solution.py:491

commit v4 on v3

--- a/solution.py
+++ b/solution.py
@@ -30,6 +30,10 @@
 
 def step_to(i, k, n):
     return i ^ k if n & (n - 1) == 0 else lax.rem(i + k, n)
+
+
+def steps_between(i, t, n):
+    return i ^ t if n & (n - 1) == 0 else lax.rem(t - i + n, n)
 
 
 def step_from(i, k, n):
@@ -372,12 +376,25 @@
         return 2 * step_to(z, k // 2, pairs) + (core ^ (k % 2))
 
     if n_dp * n_ex <= DIRECT:
+        def give(q, f):
+            k = 2 * steps_between(z, f // 2, pairs) + (core ^ (f % 2))
+            send(
+                back_out.at[k, q], back_in.at[k * n_dp + steps_between(p, q, n_dp)],
+                b1_sem.at[0], b1_sem.at[1], q, f,
+            )
+
+        for f in range(2):
+            @pl.when((p > 0) | (e != f))
+            def _(f=f):
+                give(0, f)
+
         for r in range(n_ex * n_dp - 1, 0, -1):
-            q = step_to(p, r % n_dp, n_dp)
-            send(
-                back_out.at[r // n_dp, q], back_in.at[r], b1_sem.at[0], b1_sem.at[1],
-                q, far(r // n_dp),
-            )
+            q, f = step_to(p, r % n_dp, n_dp), far(r // n_dp)
+
+            @pl.when((q > 0) | (f > 1))
+            def _(q=q, f=f):
+                give(q, f)
+
         back_in[0] = back_out[0, p]
         weight_grads()
         arrived = back_in.at[1:n_ex * n_dp]

time: 37.5 us -> 36.6 us (0.976)
  Pallas kernels: 36.6 us -> 35.8 us
    pallas_call x1, Pallas kernels: 32.7 us -> 32 us  [per_device(): pl.pallas_call(functools.partial(exchange_kernel, n_dp, n_ex, batches), o...]
where the time goes in v4:
time: 36.6 us; the launch traced here: 36.4 us
  Pallas kernels  35.8 us (98%)
  between operations  0.64 us (2%)
    pallas_call x1, Pallas kernels, per_device(): pl.pallas_call(functools.partial(exchange_kernel, n_dp, n_ex, batches), o...  32 us
    pallas_call x1, Pallas kernels, per_device(): pl.pallas_call(store_kernel, in_specs=[vm, vm], out_specs=(pl.BlockSpec(m...  3.8 us

profile of v4, /device:TPU:0, one launch (start us, length us, event | category | flops | bytes accessed | tf_op | source)
XLA Modules:
  0.0 36.4 jit_solution(10711677607513691671)
XLA Ops:
  0.6 32.0 %shard_map.77 = (f32[3,768,1024]{2,1,0:T(8,128)S(1)}, bf16[12,3072]{1,0:T(8,128)(2,1)S(1)}) custom-call(bf16[12,3072]{1,0:T(8,128)(2,1)} %og_hbm.1, bf16[12,3072]{1,0:T(8,128)(2,1)} %li_hbm.1, s32[2,12]{1,0:T(2,128)} %bitcast.2, f32[2,12]{1,0:T(2,128)} %bitcast.3, s32[3,6,8]{2,1,0:T(8,128)} %exps_hbm.1, bf16[3,768,1024]{2,1,0:T(8,128)(2,1)} %w_hbm.1), custom_call_target="tpu_custom_call" | custom-call | tf_op jit(solution)/shard_map/pallas_call | solution.py:461
  32.6 3.8 %shard_map.78 = (f32[3,768,1024]{2,1,0:T(8,128)}, bf16[12,3072]{1,0:T(8,128)(2,1)}) custom-call(f32[3,768,1024]{2,1,0:T(8,128)S(1)} %get-tuple-element.6.wg_ref, bf16[12,3072]{1,0:T(8,128)(2,1)S(1)} %get-tuple-element.7.ig_ref), custom_call_target="tpu_custom_call" | custom-call | tf_op jit(solution)/shard_map/pallas_call | solution.py:508

commit v5 on v4

--- a/solution.py
+++ b/solution.py
@@ -87,9 +87,11 @@
         og_ref, li_ref, ids_ref, prob_ref, exps_ref, xt, act, w, slab_out, slabs, x, hid_out, hid_in,
         acc, back_out, back_in, own_out, own_in,
         in_sem, s1_send, s1_recv, s2_send, s2_recv, s3_send, s3_recv, ready,
-        rs_send, rs_recv, ag_send, ag_recv, hg_sem, b1_sem, b2_sem,
-    ) = scratch[:33]
-    bufs = scratch[33:]
+        rs_send, rs_recv, ag_send, ag_recv, hg_sem, b1_sem,
+    ) = scratch[:32]
+    if n_dp * n_ex > DIRECT:
+        b2_sem = scratch[32]
+    bufs = scratch[32 + (n_dp * n_ex > DIRECT):]
     part_out, part_in, act_out, act_in = (bufs[i * n_b:(i + 1) * n_b] for i in range(4))
     p, e = lax.axis_index("dp"), lax.axis_index("expert")
     tok, width = og_hbm.shape
@@ -133,10 +135,8 @@
         def _(s=s):
             tell(barrier, p, 2 * s + other)
 
-    for copy in in_copies[:4]:
+    for copy in in_copies[:2]:
         copy.wait()
-    for copy in in_copies[5:]:
-        copy.start()
     routed = ids_ref[...] == 0
     mask = jnp.max(routed.astype(F32), axis=0, keepdims=True)
     prob = jnp.sum(jnp.where(routed, prob_ref[...], 0.0), axis=0, keepdims=True)
@@ -147,6 +147,10 @@
     hit_in = jnp.where((place == row) & (row < CAP) & mask_tall, 1.0, 0.0)
     hit_gr = jnp.where((place + CAP == row) & (row >= CAP) & mask_tall, 1.0, 0.0)
     row_prob = jnp.sum(hit_gr * prob, axis=1, keepdims=True)
+    for copy in in_copies[2:4]:
+        copy.wait()
+    for copy in in_copies[5:]:
+        copy.start()
     slots = (
         mm(hit_in.astype(BF), li_ref[...]) + row_prob * mm(hit_gr.astype(BF), og_ref[...])
     ).astype(BF)
@@ -156,13 +160,13 @@
 
     for k in range(n_dp - 1, 0, -1):
         q = step_to(p, k, n_dp)
-        send(slab_out.at[q], slabs.at[z, other, p], s1_send, s1_recv.at[k], q, partner)
+        send(slab_out.at[q], slabs.at[z, other, p], s1_send, s1_recv.at[k - 1], q, partner)
     for j in range(1, pairs):
         s = step_from(z, j, pairs)
 
         @pl.when(s < z)
         def _(s=s, j=j):
-            tell(ready.at[j], p, 2 * s + other)
+            tell(ready.at[j - 1], p, 2 * s + other)
 
     slabs[z, core, p] = slab_out[p]
 
@@ -172,7 +176,7 @@
 
             @pl.when(t < z)
             def _(t=t, j=j):
-                send(src, src, s2_send, s2_recv.at[j], p, 2 * t + other)
+                send(src, src, s2_send, s2_recv.at[j - 1], p, 2 * t + other)
 
     fine = n_dp <= 4
     if fine:
@@ -196,7 +200,7 @@
 
     for k in range(1, n_dp):
         q = step_from(p, k, n_dp)
-        wait(slabs.at[z, core, q], s1_recv.at[k])
+        wait(slabs.at[z, core, q], s1_recv.at[k - 1])
         if fine:
             forward_down(slabs.at[z, core, q])
     held = slabs.at[z, core]
@@ -208,20 +212,21 @@
 
         @pl.when(t > z)
         def _(t=t, j=j):
-            pl.semaphore_wait(ready.at[j], 1)
-            send(held, held, s2_send, s2_recv.at[j], p, 2 * t + other)
+            pl.semaphore_wait(ready.at[j - 1], 1)
+            send(held, held, s2_send, s2_recv.at[j - 1], p, 2 * t + other)
 
     def pass_on(b):
         for j in b.steps:
             if j:
                 block = slabs.at[step_from(z, j, pairs), other]
-                wait(block, s2_recv.at[j])
-                send(block, block, s3_send, s3_recv.at[j], p, partner)
+                wait(block, s2_recv.at[j - 1])
+                send(block, block, s3_send, s3_recv.at[n_b - 1], p, partner)
 
     def collect(b):
-        for j in b.steps:
-            s = step_from(z, j, pairs)
-            wait(slabs.at[s, core if j else other], s3_recv.at[j])
+        if not b.last:
+            wait(slabs.at[z, other], s3_recv.at[0])
+        else:
+            wait(slabs.at[0:len(b.steps), 0], s3_recv.at[n_b - 1])
         shape = (2 * b.padded, len(b.steps) * 16)
         src, dst = iota(shape, 1), iota(shape, 0)
         kind, r = dst // b.padded, dst % b.padded
@@ -486,13 +491,13 @@
             pltpu.VMEM((n_dp,) + packed, BF),
             pltpu.VMEM((n_dp,) + packed, BF),
             dma((8,)),
-            dma, dma((n_dp,)),
-            dma, dma((pairs,)),
-            dma, dma((pairs,)),
-            pltpu.SemaphoreType.REGULAR((pairs,)),
+            dma, dma((n_dp - 1,)),
+            dma, dma((pairs - 1,)),
+            dma, dma((n_b,)),
+            pltpu.SemaphoreType.REGULAR((pairs - 1,)),
             dma((n_b,)), dma((parts,)),
             dma((n_b,)), dma((parts,)),
-            dma((2,)), dma((2,)), dma((2,)),
+            dma((2,)), dma((2,))] + [dma((2,))] * (not direct) + [
         ]
         + [pltpu.VMEM((b.n_chunk, n_dp, b.sum_rows, b.chunk), BF) for b in batches]
         + [pltpu.VMEM((b.n_chunk, n_dp, b.sum_rows, b.chunk), BF) for b in batches]

time: 36.6 us -> 36.4 us (level)
  no operation moved by 1% of the time
where the time goes in v5:
time: 36.4 us; the launch traced here: 36.3 us
  Pallas kernels  35.6 us (98%)
  between operations  0.64 us (2%)
    pallas_call x1, Pallas kernels, per_device(): pl.pallas_call(functools.partial(exchange_kernel, n_dp, n_ex, batches), o...  31.8 us
    pallas_call x1, Pallas kernels, per_device(): pl.pallas_call(store_kernel, in_specs=[vm, vm], out_specs=(pl.BlockSpec(m...  3.8 us

profile of v5, /device:TPU:0, one launch (start us, length us, event | category | flops | bytes accessed | tf_op | source)
XLA Modules:
  0.0 36.3 jit_solution(12740492586940193671)
XLA Ops:
  0.6 31.8 %shard_map.77 = (f32[3,768,1024]{2,1,0:T(8,128)S(1)}, bf16[12,3072]{1,0:T(8,128)(2,1)S(1)}) custom-call(bf16[12,3072]{1,0:T(8,128)(2,1)} %og_hbm.1, bf16[12,3072]{1,0:T(8,128)(2,1)} %li_hbm.1, s32[2,12]{1,0:T(2,128)} %bitcast.2, f32[2,12]{1,0:T(2,128)} %bitcast.3, s32[3,6,8]{2,1,0:T(8,128)} %exps_hbm.1, bf16[3,768,1024]{2,1,0:T(8,128)(2,1)} %w_hbm.1), custom_call_target="tpu_custom_call" | custom-call | tf_op jit(solution)/shard_map/pallas_call | solution.py:466
  32.5 3.8 %shard_map.78 = (f32[3,768,1024]{2,1,0:T(8,128)}, bf16[12,3072]{1,0:T(8,128)(2,1)}) custom-call(f32[3,768,1024]{2,1,0:T(8,128)S(1)} %get-tuple-element.6.wg_ref, bf16[12,3072]{1,0:T(8,128)(2,1)S(1)} %get-tuple-element.7.ig_ref), custom_call_target="tpu_custom_call" | custom-call | tf_op jit(solution)/shard_map/pallas_call | solution.py:513
